TPU v7x, 32 devices: a whole 2x2x4 slice. The times are simulated.
32 devices in a mesh: dp: 4 (over y, core), expert: 2 (over x), group: 4 (over z).
Axes of the slice: x: 2, y: 2, z: 4, core: 2. Of those that a mesh axis runs over, the one named last changes fastest.
Arguments:
- tokens: bfloat16 [256, 7168], P(('dp', 'group')), may hold values from -6 to 6
- expert_ids: int32 [256, 8], P(('dp', 'group')), may hold values from 0 to 255, all different within a row; in each aligned block of 16 rows (0 to 15, 16 to 31, ...) at most 2 rows name the same one
- gate_values: bfloat16 [256, 8], P(('dp', 'group')), may hold values from 0.099609375 to 1
- gate_up: bfloat16 [2, 7168, 2, 2048], P('expert', None, None, 'group'), may hold values from -0.0625 to 0.0625
- down_weight: bfloat16 [2, 2048, 7168], P('expert', 'group'), may hold values from -0.125 to 0.125
- shared_gate_up: bfloat16 [7168, 2, 2048], P('expert', None, 'group'), may hold values from -0.0625 to 0.0625
- shared_down: bfloat16 [2048, 7168], P('group', 'expert'), may hold values from -0.125 to 0.125
Outputs:
- mixed: bfloat16 [256, 7168], P(('dp', 'group'), 'expert')
Inputs may be any that keep to these rules, and one draw needn't show every extreme that they name: `expert_ids`: each row names 8 different routed experts. In each aligned block of 16 rows (the rows of one device) no expert is named by more than 2 rows, and in some blocks one is named by exactly 2 rows.
All inputs are finite; a program needn't handle non-finite values.
Results may differ from a plain program's by a relative error of at most 0.028.
Values may be sent and summed in bfloat16 or wider, within the bound.
A program may use at most 128 MiB of HBM per device.

v0:
```python
import functools

import jax
import jax.numpy as jnp
from jax import lax
from jax.experimental import pallas as pl
from jax.experimental.pallas import tpu as pltpu
from jax.sharding import PartitionSpec as P

MESH = pl.DeviceIdType.MESH
BF16, F32 = jnp.bfloat16, jnp.float32
CAP = 2
LANES = 128
DEPTH = 1792


def nearest_first(count):
    order = []
    for distance in range(1, count // 2 + 1):
        for candidate in (distance, count - distance):
            if candidate not in order:
                order.append(candidate)
    return order


def batches_of(count):
    order = nearest_first(count) + [0]
    return [order[i : i + 2] for i in range(0, count, 2)]


def schedule_of(batches):
    return [(kind, b) for kind in ("pre", "fin") for b in range(len(batches))]


def silu(value):
    return value / (1.0 + jnp.exp(-value))


def kernel(
    n_expert, n_group,
    tokens, ids, gates, gate_up, down, shared_gate_up, shared_down,
    out,
    w_routed, w_down, w_shared, w_shared_down,
    x_all, x_shared, rows_all, x_routed,
    pre_own, pre_out, pre_in, term_out, term_in, routed_out, routed_in,
    routed_w_sem, down_w_sem, shared_w_sem, shared_down_w_sem, own_sem,
    x_send, x_recv, rows_send, rows_recv, pre_send, pre_recv,
    term_send, term_recv, routed_send, routed_recv,
):
    me_e, me_g = lax.axis_index("expert"), lax.axis_index("group")
    n_tokens, width = tokens.shape
    columns = x_all.shape[2]
    units = w_shared_down.shape[0]
    tiles = units // LANES
    pair = 2 if tiles % 2 == 0 else 1
    order = nearest_first(n_group)
    batches = batches_of(n_group)

    def expert_at(distance):
        return lax.rem(me_e + n_expert + distance, n_expert)

    def group_at(distance):
        return lax.rem(me_g + n_group + distance, n_group)

    def weight_copies(source, target, sem):
        depth = min(DEPTH, source.shape[0])
        groups = []
        for n in range(source.shape[0] // depth):
            rows = pl.ds(n * depth, depth)
            groups.append([
                pltpu.make_async_copy(
                    source.at[rows, pl.ds(c * LANES, LANES)], target.at[c, rows], sem.at[n, c]
                )
                for c in range(tiles)
            ])
        return groups

    shared_groups = weight_copies(
        shared_gate_up.reshape(2 * columns, units), w_shared, shared_w_sem
    )
    routed_groups = weight_copies(gate_up.reshape(2 * width, units), w_routed, routed_w_sem)
    part = units // 4
    shared_down_copies = [
        pltpu.make_async_copy(
            shared_down.at[pl.ds(i * part, part)], w_shared_down.at[pl.ds(i * part, part)],
            shared_down_w_sem.at[i],
        )
        for i in range(4)
    ]
    down_copies = [
        pltpu.make_async_copy(
            down.at[0, :, pl.ds(pl.multiple_of(expert_at(-d) * columns, LANES), columns)],
            w_down.at[d],
            down_w_sem.at[d],
        )
        for d in range(n_expert)
    ]
    own_columns = pl.ds(pl.multiple_of(me_e * columns, LANES), columns)
    own_copy = pltpu.make_async_copy(tokens.at[:, own_columns], x_all.at[0], own_sem)
    own_copy.start()
    for group in shared_groups:
        for copy in group:
            copy.start()
    for copy in shared_down_copies:
        copy.start()
    for group in routed_groups:
        for copy in group:
            copy.start()
    for copy in down_copies:
        copy.start()

    barrier = pltpu.get_barrier_semaphore()
    for d in range(n_expert):
        for s in range(n_group):
            if d or s:
                pl.semaphore_signal(
                    barrier, inc=1,
                    device_id={"expert": expert_at(d), "group": group_at(s)},
                    device_id_type=MESH,
                )

    before = (
        lax.broadcasted_iota(jnp.int32, (n_tokens, n_tokens), 0)
        < lax.broadcasted_iota(jnp.int32, (n_tokens, n_tokens), 1)
    ).astype(BF16)
    ranks = lax.broadcasted_iota(jnp.int32, (8, n_tokens), 0).astype(F32)

    def picked_by(expert):
        chosen = ids[...] == expert
        named = jnp.sum(jnp.where(chosen, 1.0, 0.0), axis=0, keepdims=True)
        value = jnp.sum(jnp.where(chosen, gates[...].astype(F32), 0.0), axis=0, keepdims=True)
        named = jnp.broadcast_to(named, (8, n_tokens))
        rank = jnp.dot(named.astype(BF16), before, preferred_element_type=F32)
        picked = jnp.where((named > 0.5) & (jnp.abs(rank - ranks) < 0.5), 1.0, 0.0)
        return picked, jnp.broadcast_to(value, (8, n_tokens))

    picked, _ = picked_by(me_e)
    selected = jnp.dot(picked.astype(BF16), tokens[...], preferred_element_type=F32)
    rows_all[0] = selected[:CAP].astype(BF16)

    pl.semaphore_wait(barrier, n_expert * n_group - 1)

    x_copies, rows_copies = {}, {}
    relayed = n_group == 4
    for s in [1, 3] if relayed else order:
        x_copies[s] = pltpu.make_async_remote_copy(
            src_ref=tokens.at[:, own_columns], dst_ref=x_all.at[s],
            send_sem=x_send.at[s], recv_sem=x_recv.at[s],
            device_id={"group": group_at(s)}, device_id_type=MESH,
        )
        x_copies[s].start()
    x_arrivals = {s: [copy] for s, copy in x_copies.items()}
    if relayed:
        half = columns // 2
        for s, sem, first in ((1, 2, 0), (3, 0, half)):
            x_copies[s].wait_recv()
            at = pl.ds(first, half)
            relay = pltpu.make_async_remote_copy(
                src_ref=x_all.at[s, :, at], dst_ref=x_all.at[2, :, at],
                send_sem=x_send.at[sem], recv_sem=x_recv.at[sem],
                device_id={"group": group_at(s)}, device_id_type=MESH,
            )
            relay.start()
            x_arrivals[s] = []
            x_arrivals.setdefault(2, []).append(relay)
            x_copies["relay", s] = relay
    for s in order:
        rows_copies[s] = pltpu.make_async_remote_copy(
            src_ref=rows_all.at[0], dst_ref=rows_all.at[s],
            send_sem=rows_send.at[s], recv_sem=rows_recv.at[s],
            device_id={"group": group_at(s)}, device_id_type=MESH,
        )
        rows_copies[s].start()

    feature = lax.broadcasted_iota(jnp.int32, (LANES, 4 * LANES), 0)
    place = lax.broadcasted_iota(jnp.int32, (LANES, 4 * LANES), 1)
    spread = (
        (place == 2 * feature) | (place == 2 * feature + 1 + 2 * LANES)
    ).astype(BF16)

    def project(x, weights, groups, wait):
        depth = min(DEPTH, x.shape[1])
        totals = [None] * (tiles // pair)
        for n in range(x.shape[1] // depth):
            if wait:
                for copy in groups[n]:
                    copy.wait()
            rows = pl.ds(n * depth, depth)
            x_part = x[:, pl.ds(n * depth, depth)]
            for p in range(tiles // pair):
                block = [weights[p * pair + i, rows] for i in range(pair)]
                block = jnp.concatenate(block, axis=1) if pair > 1 else block[0]
                product = jnp.dot(x_part, block, preferred_element_type=F32)
                totals[p] = product if totals[p] is None else totals[p] + product
        return totals

    pre_copies, term_copies = {}, {}
    piece = columns // 7 if columns % (7 * LANES) == 0 else columns
    shared_waits = list(shared_groups)

    def pre(b):
        members = batches[b]
        n_rows = len(members) * n_tokens
        for s in members:
            if s:
                for copy in x_arrivals[s]:
                    copy.wait_recv()
            else:
                own_copy.wait()

        def expand(j, carry):
            source = pl.ds(pl.multiple_of(j * LANES, LANES), LANES)
            target = pl.ds(pl.multiple_of(j * 2 * LANES, 2 * LANES), 2 * LANES)
            part = jnp.concatenate([x_all[s, :, source] for s in members], axis=0)
            both = jnp.dot(part, spread, preferred_element_type=F32).astype(BF16)
            x_shared[:n_rows, target] = both[:, : 2 * LANES]
            x_shared[n_rows : 2 * n_rows, target] = both[:, 2 * LANES :]
            return carry

        lax.fori_loop(0, columns // LANES, expand, 0, unroll=True)
        totals = project(x_shared.at[: 2 * n_rows], w_shared, shared_groups, bool(shared_waits))
        shared_waits.clear()
        for p, total in enumerate(totals):
            at = pl.ds(p * pair * LANES, pair * LANES)
            pre_own[b, : 2 * n_rows, at] = total
            pre_out[b, : 2 * n_rows, at] = total.astype(BF16)
        pre_copies[b] = []
        for d in range(1, n_expert):
            rows = pl.ds(0, 2 * n_rows)
            copy = pltpu.make_async_remote_copy(
                src_ref=pre_out.at[b, rows], dst_ref=pre_in.at[d - 1, b, rows],
                send_sem=pre_send.at[d - 1, b], recv_sem=pre_recv.at[d - 1, b],
                device_id={"expert": expert_at(d)}, device_id_type=MESH,
            )
            copy.start()
            pre_copies[b].append(copy)

    down_waits = list(shared_down_copies)

    def fin(b):
        members = batches[b]
        n_rows = len(members) * n_tokens
        for copy in pre_copies[b]:
            copy.wait_recv()
        total = pre_own[b, : 2 * n_rows]
        for d in range(1, n_expert):
            total = total + pre_in[d - 1, b, : 2 * n_rows].astype(F32)
        hidden = (silu(total[:n_rows]) * total[n_rows:]).astype(BF16)
        for copy in down_waits:
            copy.wait()
        down_waits.clear()
        for n in range(columns // piece):
            at = pl.ds(n * piece, piece)
            term = jnp.dot(hidden, w_shared_down[:, at], preferred_element_type=F32).astype(BF16)
            for i, s in enumerate(members):
                rows = term[i * n_tokens : (i + 1) * n_tokens]
                if s:
                    term_out[s, :, at] = rows
                else:
                    term_in[0, :, at] = rows
        for s in members:
            if s:
                term_copies[s] = pltpu.make_async_remote_copy(
                    src_ref=term_out.at[s], dst_ref=term_in.at[s],
                    send_sem=term_send.at[s], recv_sem=term_recv.at[s],
                    device_id={"group": group_at(-s)}, device_id_type=MESH,
                )
                term_copies[s].start()

    for kind, b in schedule_of(batches):
        (pre if kind == "pre" else fin)(b)

    for s in order:
        rows_copies[s].wait_recv()
    routed_rows = n_group * CAP

    def expand_rows(j, carry):
        source = pl.ds(pl.multiple_of(j * LANES, LANES), LANES)
        target = pl.ds(pl.multiple_of(j * 2 * LANES, 2 * LANES), 2 * LANES)
        part = rows_all[:, :, source].reshape(routed_rows, LANES)
        both = jnp.dot(part, spread, preferred_element_type=F32).astype(BF16)
        x_routed[:routed_rows, target] = both[:, : 2 * LANES]
        x_routed[routed_rows:, target] = both[:, 2 * LANES :]
        return carry

    lax.fori_loop(0, width // LANES, expand_rows, 0, unroll=True)
    totals = project(x_routed, w_routed, routed_groups, True)
    hidden = jnp.concatenate(
        [(silu(t[:routed_rows]) * t[routed_rows:]).astype(BF16) for t in totals], axis=1
    )
    routed_copies = {}
    for d in reversed(range(n_expert)):
        down_copies[d].wait()
        for n in range(columns // piece):
            at = pl.ds(n * piece, piece)
            term = jnp.dot(hidden, w_down[d, :, at], preferred_element_type=F32).astype(BF16)
            for s in range(n_group):
                rows = term[s * CAP : (s + 1) * CAP]
                if d or s:
                    routed_out[d, s, :, at] = rows
                else:
                    routed_in[0, 0, :, at] = rows
        for s in order + [0]:
            if d or s:
                routed_copies[d, s] = pltpu.make_async_remote_copy(
                    src_ref=routed_out.at[d, s], dst_ref=routed_in.at[d, s],
                    send_sem=routed_send.at[d, s], recv_sem=routed_recv.at[d, s],
                    device_id={"expert": expert_at(-d), "group": group_at(-s)},
                    device_id_type=MESH,
                )
                routed_copies[d, s].start()

    identity = (
        lax.broadcasted_iota(jnp.int32, (n_tokens, n_tokens), 0)
        == lax.broadcasted_iota(jnp.int32, (n_tokens, n_tokens), 1)
    ).astype(BF16)
    weights = []
    for d in range(n_expert):
        picked, value = picked_by(expert_at(d))
        weights.append(lax.dot_general(
            identity, (picked * value).astype(BF16), (((1,), (1,)), ((), ())),
            preferred_element_type=F32,
        ))
    for s in order:
        term_copies[s].wait_recv()
    for copy in routed_copies.values():
        copy.wait_recv()
    for n in range(columns // piece):
        at = pl.ds(n * piece, piece)
        total = term_in[0, :, at].astype(F32)
        for s in order:
            total = total + term_in[s, :, at].astype(F32)
        for d in range(n_expert):
            rows = routed_in[d, 0, :, at].astype(F32)
            for s in range(1, n_group):
                rows = rows + routed_in[d, s, :, at].astype(F32)
            for r in range(CAP):
                total = total + weights[d][:, r : r + 1] * rows[r : r + 1]
        out[:, at] = total.astype(BF16)

    for copies in (x_copies, rows_copies, term_copies, routed_copies):
        for copy in copies.values():
            copy.wait_send()
    for copies in pre_copies.values():
        for copy in copies:
            copy.wait_send()


def per_device(n_expert, n_group, tokens, ids, gates, gate_up, down, shared_gate_up, shared_down):
    n_tokens, width = tokens.shape
    columns, _, units = shared_gate_up.shape
    tiles = units // LANES
    batches = batches_of(n_group)
    n_batches = len(batches)
    n_rows = max(len(members) for members in batches) * n_tokens
    vmem, dma = pltpu.VMEM, pltpu.SemaphoreType.DMA
    in_vmem, in_hbm = pl.BlockSpec(memory_space=pltpu.VMEM), pl.BlockSpec(memory_space=pltpu.HBM)
    return pl.pallas_call(
        functools.partial(kernel, n_expert, n_group),
        out_shape=jax.ShapeDtypeStruct((n_tokens, columns), BF16),
        in_specs=[in_vmem] * 3 + [in_hbm] * 4,
        out_specs=in_vmem,
        scratch_shapes=[
            vmem((tiles, 2 * width, LANES), BF16),
            vmem((n_expert, units, columns), BF16),
            vmem((tiles, 2 * columns, LANES), BF16),
            vmem((units, columns), BF16),
            vmem((n_group, n_tokens, columns), BF16),
            vmem((2 * n_rows, 2 * columns), BF16),
            vmem((n_group, CAP, width), BF16),
            vmem((2 * n_group * CAP, 2 * width), BF16),
            vmem((n_batches, 2 * n_rows, units), F32),
            vmem((n_batches, 2 * n_rows, units), BF16),
            vmem((max(1, n_expert - 1), n_batches, 2 * n_rows, units), BF16),
            vmem((n_group, n_tokens, columns), BF16),
            vmem((n_group, n_tokens, columns), BF16),
            vmem((n_expert, n_group, CAP, columns), BF16),
            vmem((n_expert, n_group, CAP, columns), BF16),
            dma((max(1, 2 * width // DEPTH), tiles)),
            dma((n_expert,)),
            dma((max(1, 2 * columns // DEPTH), tiles)),
            dma((4,)),
            dma,
            dma((n_group,)), dma((n_group,)),
            dma((n_group,)), dma((n_group,)),
            dma((max(1, n_expert - 1), n_batches)), dma((max(1, n_expert - 1), n_batches)),
            dma((n_group,)), dma((n_group,)),
            dma((n_expert, n_group)), dma((n_expert, n_group)),
        ],
        compiler_params=pltpu.CompilerParams(
            collective_id=0, has_side_effects=True, vmem_limit_bytes=60 * 2**20
        ),
    )(tokens, ids.T, gates.T, gate_up, down, shared_gate_up, shared_down)


def solution(mesh):
    in_specs = (
        P(("dp", "group"), None),
        P(("dp", "group"), None),
        P(("dp", "group"), None),
        P("expert", None, None, "group"),
        P("expert", "group", None),
        P("expert", None, "group"),
        P("group", "expert"),
    )
    return jax.shard_map(
        functools.partial(per_device, mesh.shape["expert"], mesh.shape["group"]),
        mesh=mesh, in_specs=in_specs, out_specs=P(("dp", "group"), "expert"), check_vma=False,
    )
```

profile of v0, /device:TPU:0, one launch (start us, length us, event | category | flops | bytes accessed | tf_op | source)
XLA Modules:
  0.0 37.5 jit_solution(10662949284057846283)
XLA Ops:
  0.0 35.9 %shard_map.73 = bf16[16,3584]{1,0:T(8,128)(2,1)} custom-call(bf16[16,7168]{1,0:T(8,128)(2,1)} %tokens.1, s32[8,16]{1,0:T(8,128)} %bitcast.2, bf16[8,16]{1,0:T(8,128)(2,1)} %bitcast.3, bf16[1,7168,2,512]{3,2,1,0:T(2,128)(2,1)} %gate_up.1, bf16[1,512,7168]{2,1,0:T(8,128)(2,1)} %down.1, bf16[3584,2,512]{2,1,0:T(2,128)(2,1)} %shared_gate_up.1, ...), custom_call_target="tpu_custom_call" | custom-call | tf_op jit(solution)/shard_map/pallas_call | solution.py:358
  35.9 1.6 %copy.9 = bf16[16,3584]{1,0:T(8,128)(2,1)} copy(bf16[16,3584]{1,0:T(8,128)(2,1)} %shard_map.73) | data formatting | bytes 229376
where the time goes:
time: 37.6 us; the launch traced here: 37.5 us
  Pallas kernels  35.9 us (95%)
  local copies, waits for them, and re-layouts  1.55 us (4%)
    pallas_call x1, Pallas kernels, per_device(): pl.pallas_call(functools.partial(kernel, n_expert, n_group), out_shape=ja...  35.9 us
    unnamed x1, local copies, waits for them, and re-layouts  1.55 us

commit v1 on v0

v1 whole, which is shorter than its diff:
```python
import functools

import jax
import jax.numpy as jnp
from jax import lax
from jax.experimental import pallas as pl
from jax.experimental.pallas import tpu as pltpu
from jax.sharding import PartitionSpec as P

MESH = pl.DeviceIdType.MESH
BF16, F32 = jnp.bfloat16, jnp.float32
CAP = 2
LANES = 128
DEPTH = 1792
scope = jax.named_scope


def line_order(count):
    orders = []
    for me in range(count):
        others = [j for j in range(count) if j != me]
        others.sort(key=lambda j: (abs(j - me), abs(2 * j - (count - 1))))
        orders.append([me] + others)
    return [[orders[me][k] for me in range(count)] for k in range(count)]


def choose(table, me):
    value = jnp.int32(0)
    for j, entry in enumerate(table):
        value = value + jnp.where(me == j, entry, 0)
    return value


def silu(value):
    return value / (1.0 + jnp.exp(-value))


def kernel(
    n_expert, n_group,
    tokens, ids_hbm, gates_hbm, gate_up, down, shared_gate_up, shared_down,
    out,
    w_routed, w_down, w_shared, w_shared_down,
    ids_all, gates,
    x_all, x_shared, rows_out, rows_all, x_routed,
    pre_own, pre_out, pre_in, term_out, term_in, routed_out, routed_in,
    routed_w_sem, down_w_sem, shared_w_sem, shared_down_w_sem, own_sem, ids_sem, gates_sem,
    x_send, x_recv, relay_send, ids_send, ids_recv, rows_send, rows_recv, pre_send, pre_recv,
    term_send, term_recv, routed_send, routed_recv,
):
    me_e, me_g = lax.axis_index("expert"), lax.axis_index("group")
    n_tokens, width = tokens.shape
    columns = x_all.shape[2]
    units = w_shared_down.shape[0]
    tiles = units // LANES
    pair = 2 if tiles % 2 == 0 else 1
    parts = 2 if columns % (2 * LANES) == 0 else 1
    part = columns // parts
    chunks = [pl.ds(c * part, part) for c in range(parts)]
    sources = [choose(table, me_g) for table in line_order(n_group)]

    def expert_at(distance):
        return lax.rem(me_e + n_expert + distance, n_expert)

    def group_at(distance):
        return lax.rem(me_g + n_group + distance, n_group)

    barrier = pltpu.get_barrier_semaphore()
    for d in range(n_expert):
        for s in range(n_group):
            if d or s:
                pl.semaphore_signal(
                    barrier, inc=1,
                    device_id={"expert": expert_at(d), "group": group_at(s)},
                    device_id_type=MESH,
                )

    own_columns = pl.ds(pl.multiple_of(me_e * columns, LANES), columns)
    own_copy = pltpu.make_async_copy(tokens.at[:, own_columns], x_all.at[me_g], own_sem)
    ids_copy = pltpu.make_async_copy(ids_hbm, ids_all.at[me_g], ids_sem)
    gates_copy = pltpu.make_async_copy(gates_hbm, gates, gates_sem)
    for copy in (own_copy, ids_copy, gates_copy):
        copy.start()

    def weight_copies(source, target, sem):
        depth = min(DEPTH, source.shape[0])
        groups = []
        for n in range(source.shape[0] // depth):
            rows = pl.ds(n * depth, depth)
            groups.append([
                pltpu.make_async_copy(
                    source.at[rows, pl.ds(c * LANES, LANES)], target.at[c, rows], sem.at[n, c]
                )
                for c in range(tiles)
            ])
        return groups

    shared_groups = weight_copies(
        shared_gate_up.reshape(2 * columns, units), w_shared, shared_w_sem
    )
    routed_groups = weight_copies(gate_up.reshape(2 * width, units), w_routed, routed_w_sem)
    shared_down_copy = pltpu.make_async_copy(shared_down, w_shared_down, shared_down_w_sem)
    down_copies = [
        pltpu.make_async_copy(
            down.at[0, :, pl.ds(pl.multiple_of(expert_at(-d) * columns, LANES), columns)],
            w_down.at[d],
            down_w_sem.at[d],
        )
        for d in range(n_expert)
    ]
    with scope("own"):
        own_copy.wait()
    for group in shared_groups:
        for copy in group:
            copy.start()
    shared_down_copy.start()
    with scope("bar"):
        pl.semaphore_wait(barrier, n_expert * n_group - 1)

    def x_copy(source, target, c, send_sem):
        return pltpu.make_async_remote_copy(
            src_ref=x_all.at[source, :, chunks[c]], dst_ref=x_all.at[source, :, chunks[c]],
            send_sem=send_sem, recv_sem=x_recv.at[source, c],
            device_id={"group": target}, device_id_type=MESH,
        )

    has_left, has_right = me_g > 0, me_g < n_group - 1
    sends = []
    for step, exists in ((-1, has_left), (1, has_right)):
        for c in range(parts):
            copy = x_copy(me_g, me_g + step, c, x_send.at[max(step, 0), c])
            pl.when(exists)(copy.start)
            sends.append((exists, copy))

    with scope("ids"):
        ids_copy.wait()
    ids_copies = []
    for s in range(1, n_group):
        copy = pltpu.make_async_remote_copy(
            src_ref=ids_all.at[me_g], dst_ref=ids_all.at[me_g],
            send_sem=ids_send.at[s], recv_sem=ids_recv.at[s],
            device_id={"group": group_at(s)}, device_id_type=MESH,
        )
        copy.start()
        ids_copies.append(copy)

    before = (
        lax.broadcasted_iota(jnp.int32, (n_tokens, n_tokens), 0)
        < lax.broadcasted_iota(jnp.int32, (n_tokens, n_tokens), 1)
    ).astype(BF16)
    ranks = lax.broadcasted_iota(jnp.int32, (8, n_tokens), 0).astype(F32)

    def picked_by(ids, expert):
        chosen = ids == expert
        named = jnp.sum(jnp.where(chosen, 1.0, 0.0), axis=0, keepdims=True)
        named = jnp.broadcast_to(named, (8, n_tokens))
        rank = jnp.dot(named.astype(BF16), before, preferred_element_type=F32)
        picked = jnp.where((named > 0.5) & (jnp.abs(rank - ranks) < 0.5), 1.0, 0.0)
        return picked, chosen

    feature = lax.broadcasted_iota(jnp.int32, (LANES, 4 * LANES), 0)
    place = lax.broadcasted_iota(jnp.int32, (LANES, 4 * LANES), 1)
    spread = (
        (place == 2 * feature) | (place == 2 * feature + 1 + 2 * LANES)
    ).astype(BF16)

    def expand(pieces, target):
        rows = pieces[0].shape[0]
        stacked = jnp.concatenate(pieces, axis=0).astype(BF16)
        both = jnp.dot(stacked, spread, preferred_element_type=F32).astype(BF16)
        for j in range(len(pieces)):
            at = pl.ds(j * 2 * LANES, 2 * LANES)
            target[:rows, at] = both[j * rows : (j + 1) * rows, : 2 * LANES]
            target[rows:, at] = both[j * rows : (j + 1) * rows, 2 * LANES :]

    def project(x, weights, groups, wait):
        depth = min(DEPTH, x.shape[1]) if wait else x.shape[1]
        totals = [None] * (tiles // pair)
        for n in range(x.shape[1] // depth):
            if wait:
                with scope(f"w{n}"):
                    for copy in groups[n]:
                        copy.wait()
            rows = pl.ds(n * depth, depth)
            x_part = x[:, pl.ds(n * depth, depth)]
            for p in range(tiles // pair):
                block = [weights[p * pair + i, rows] for i in range(pair)]
                block = jnp.concatenate(block, axis=1) if pair > 1 else block[0]
                product = jnp.dot(x_part, block, preferred_element_type=F32)
                totals[p] = product if totals[p] is None else totals[p] + product
        return totals

    pre_copies = {}

    def pre(k):
        source = sources[k]
        with scope(f"exp{k}"):
          expand([x_all[source, :, pl.ds(j * LANES, LANES)] for j in range(columns // LANES)], x_shared)
        with scope(f"proj{k}"):
            totals = project(x_shared, w_shared, shared_groups, k == 0)
        for p, total in enumerate(totals):
            at = pl.ds(p * pair * LANES, pair * LANES)
            pre_own[k, :, at] = total
            pre_out[k, :, at] = total.astype(BF16)
        pre_copies[k] = []
        for d in range(1, n_expert):
            copy = pltpu.make_async_remote_copy(
                src_ref=pre_out.at[k], dst_ref=pre_in.at[d - 1, k],
                send_sem=pre_send.at[d - 1, k], recv_sem=pre_recv.at[d - 1, k],
                device_id={"expert": expert_at(d)}, device_id_type=MESH,
            )
            copy.start()
            pre_copies[k].append(copy)

    term_copies = []

    def fin(k):
        with scope(f"prew{k}"):
            for copy in pre_copies[k]:
                copy.wait_recv()
        total = pre_own[k]
        for d in range(1, n_expert):
            total = total + pre_in[d - 1, k].astype(F32)
        hidden = (silu(total[:n_tokens]) * total[n_tokens:]).astype(BF16)
        for c in range(parts):
            term = jnp.dot(hidden, w_shared_down[:, chunks[c]], preferred_element_type=F32)
            if k:
                term_out[k, :, chunks[c]] = term.astype(BF16)
                copy = pltpu.make_async_remote_copy(
                    src_ref=term_out.at[k, :, chunks[c]], dst_ref=term_in.at[me_g, :, chunks[c]],
                    send_sem=term_send.at[k, c], recv_sem=term_recv.at[me_g, c],
                    device_id={"group": sources[k]}, device_id_type=MESH,
                )
                copy.start()
                term_copies.append(copy)
            else:
                term_in[me_g, :, chunks[c]] = term.astype(BF16)

    pre(0)

    for group in routed_groups:
        for copy in group:
            copy.start()
    for copy in down_copies:
        copy.start()

    relays = []

    def arrive(distance):
        for c in range(parts):
            for side in (0, 1):
                source = me_g + distance if side else me_g - distance
                target = me_g - 1 if side else me_g + 1
                exists = source < n_group if side else source >= 0
                passed = exists & (target >= 0 if side else target < n_group)
                relay = x_copy(source, target, c, relay_send.at[side, distance - 1, c])
                with scope(f"x{distance}{side}{c}"):
                    pl.when(exists)(relay.wait_recv)
                pl.when(passed)(relay.start)
                relays.append((passed, relay))

    rows_copies = []

    def select():
        for copy in ids_copies:
            copy.wait_recv()
        for s in range(n_group):
            source = group_at(-s)
            picked = jnp.concatenate(
                [picked_by(ids_all[source], expert_at(d))[0] for d in range(n_expert)], axis=0
            ).astype(BF16)
            rows = jnp.dot(picked, x_all[source], preferred_element_type=F32)
            for d in range(n_expert):
                target = rows_out.at[d, s] if d else rows_all.at[me_e, s]
                target[...] = rows[d * 8 : d * 8 + CAP].astype(BF16)
        for d in range(1, n_expert):
            copy = pltpu.make_async_remote_copy(
                src_ref=rows_out.at[d], dst_ref=rows_all.at[me_e],
                send_sem=rows_send.at[d], recv_sem=rows_recv.at[d],
                device_id={"expert": expert_at(d)}, device_id_type=MESH,
            )
            copy.start()
            rows_copies.append(copy)

    shared_down_waited = False
    for k in range(1, n_group):
        arrive(k)
        if k == n_group - 1:
            with scope("select"):
                select()
        pre(k)
        if k > 1:
            if not shared_down_waited:
                shared_down_copy.wait()
                shared_down_waited = True
            fin(k - 1)
    if not shared_down_waited:
        shared_down_copy.wait()

    with scope("rows"):
        for copy in rows_copies:
            copy.wait_recv()
    routed_rows = n_group * CAP
    with scope("rexp"):
      expand(
        [
            rows_all[h, :, :, pl.ds(j * LANES, LANES)].reshape(routed_rows, LANES).astype(F32)
            for h in range(n_expert)
            for j in range(columns // LANES)
        ],
        x_routed,
    )
    if n_group > 1:
        fin(n_group - 1)
    with scope("rproj"):
        totals = project(x_routed, w_routed, routed_groups, True)
    routed_hidden = jnp.concatenate(
        [(silu(t[:routed_rows]) * t[routed_rows:]).astype(BF16) for t in totals], axis=1
    )

    routed_copies = []
    for d in reversed(range(n_expert)):
        with scope(f"dw{d}"):
            down_copies[d].wait()
        for c in range(parts):
            term = jnp.dot(
                routed_hidden, w_down[d, :, chunks[c]], preferred_element_type=F32
            ).astype(BF16)
            for s in range(n_group):
                rows = term[s * CAP : (s + 1) * CAP]
                if d or s:
                    routed_out[d, s, :, chunks[c]] = rows
                else:
                    routed_in[0, 0, :, chunks[c]] = rows
        for s in list(range(1, n_group)) + [0]:
            if d or s:
                copy = pltpu.make_async_remote_copy(
                    src_ref=routed_out.at[d, s], dst_ref=routed_in.at[d, s],
                    send_sem=routed_send.at[d, s], recv_sem=routed_recv.at[d, s],
                    device_id={"expert": expert_at(-d), "group": group_at(-s)},
                    device_id_type=MESH,
                )
                copy.start()
                routed_copies.append(copy)
    fin(0)

    identity = (
        lax.broadcasted_iota(jnp.int32, (n_tokens, n_tokens), 0)
        == lax.broadcasted_iota(jnp.int32, (n_tokens, n_tokens), 1)
    ).astype(BF16)
    gates_copy.wait()
    weights = []
    for d in range(n_expert):
        picked, chosen = picked_by(ids_all[me_g], expert_at(d))
        value = jnp.sum(jnp.where(chosen, gates[...].astype(F32), 0.0), axis=0, keepdims=True)
        weights.append(lax.dot_general(
            identity, (picked * value).astype(BF16), (((1,), (1,)), ((), ())),
            preferred_element_type=F32,
        ))
    with scope("routed"):
        for copy in routed_copies:
            copy.wait_recv()
    for c in range(parts):
        for s in range(n_group):
            copy = pltpu.make_async_remote_copy(
                src_ref=term_out.at[0, :, chunks[c]], dst_ref=term_in.at[s, :, chunks[c]],
                send_sem=term_send.at[0, c], recv_sem=term_recv.at[s, c],
                device_id={"group": group_at(1)}, device_id_type=MESH,
            )
            with scope(f"term{c}{s}"):
                pl.when(me_g != s)(copy.wait_recv)
        at = chunks[c]
        total = term_in[0, :, at].astype(F32)
        for s in range(1, n_group):
            total = total + term_in[s, :, at].astype(F32)
        for d in range(n_expert):
            rows = routed_in[d, 0, :, at].astype(F32)
            for s in range(1, n_group):
                rows = rows + routed_in[d, s, :, at].astype(F32)
            for r in range(CAP):
                total = total + weights[d][:, r : r + 1] * rows[r : r + 1]
        out[:, at] = total.astype(BF16)

    with scope("sendw"):
      for exists, copy in sends + relays:
        pl.when(exists)(copy.wait_send)
    for copy in ids_copies + rows_copies + term_copies + routed_copies:
        copy.wait_send()
    for copies in pre_copies.values():
        for copy in copies:
            copy.wait_send()


def per_device(n_expert, n_group, tokens, ids, gates, gate_up, down, shared_gate_up, shared_down):
    n_tokens, width = tokens.shape
    columns, _, units = shared_gate_up.shape
    tiles = units // LANES
    top = ids.shape[1]
    parts = 2 if columns % (2 * LANES) == 0 else 1
    vmem, dma = pltpu.VMEM, pltpu.SemaphoreType.DMA
    in_vmem, in_hbm = pl.BlockSpec(memory_space=pltpu.VMEM), pl.BlockSpec(memory_space=pltpu.HBM)
    return pl.pallas_call(
        functools.partial(kernel, n_expert, n_group),
        out_shape=jax.ShapeDtypeStruct((n_tokens, columns), BF16),
        in_specs=[in_hbm] * 7,
        out_specs=in_vmem,
        scratch_shapes=[
            vmem((tiles, 2 * width, LANES), BF16),
            vmem((n_expert, units, columns), BF16),
            vmem((tiles, 2 * columns, LANES), BF16),
            vmem((units, columns), BF16),
            vmem((n_group, top, n_tokens), jnp.int32),
            vmem((top, n_tokens), BF16),
            vmem((n_group, n_tokens, columns), BF16),
            vmem((2 * n_tokens, 2 * columns), BF16),
            vmem((n_expert, n_group, CAP, columns), BF16),
            vmem((n_expert, n_group, CAP, columns), BF16),
            vmem((2 * n_group * CAP, 2 * width), BF16),
            vmem((n_group, 2 * n_tokens, units), F32),
            vmem((n_group, 2 * n_tokens, units), BF16),
            vmem((max(1, n_expert - 1), n_group, 2 * n_tokens, units), BF16),
            vmem((n_group, n_tokens, columns), BF16),
            vmem((n_group, n_tokens, columns), BF16),
            vmem((n_expert, n_group, CAP, columns), BF16),
            vmem((n_expert, n_group, CAP, columns), BF16),
            dma((max(1, 2 * width // DEPTH), tiles)),
            dma((n_expert,)),
            dma((max(1, 2 * columns // DEPTH), tiles)),
            dma, dma, dma, dma,
            dma((2, parts)), dma((n_group, parts)), dma((2, n_group, parts)),
            dma((n_group,)), dma((n_group,)),
            dma((n_expert,)), dma((n_expert,)),
            dma((max(1, n_expert - 1), n_group)), dma((max(1, n_expert - 1), n_group)),
            dma((n_group, parts)), dma((n_group, parts)),
            dma((n_expert, n_group)), dma((n_expert, n_group)),
        ],
        compiler_params=pltpu.CompilerParams(
            collective_id=0, has_side_effects=True, vmem_limit_bytes=42 * 2**20
        ),
    )(*(
        pltpu.with_memory_space_constraint(array, pltpu.HBM)
        for array in (tokens, ids.T, gates.T, gate_up, down, shared_gate_up, shared_down)
    ))


def solution(mesh):
    in_specs = (
        P(("dp", "group"), None),
        P(("dp", "group"), None),
        P(("dp", "group"), None),
        P("expert", None, None, "group"),
        P("expert", "group", None),
        P("expert", None, "group"),
        P("group", "expert"),
    )
    return jax.shard_map(
        functools.partial(per_device, mesh.shape["expert"], mesh.shape["group"]),
        mesh=mesh, in_specs=in_specs, out_specs=P(("dp", "group"), "expert"), check_vma=False,
    )
```

time: 37.6 us -> 31.8 us (0.85)
  Pallas kernels: 35.9 us -> 31 us
  local copies, waits for them, and re-layouts: 1.55 us -> 0.65 us
    pallas_call x1, Pallas kernels: 35.9 us -> 31 us  [per_device(): pl.pallas_call(functools.partial(kernel, n_expert, n_group), out_shape=ja...]
    unnamed x1, local copies, waits for them, and re-layouts: 1.55 us -> 0.65 us
where the time goes in v1:
time: 31.8 us; the launch traced here: 31.6 us
  Pallas kernels  31 us (97%)
  local copies, waits for them, and re-layouts  0.65 us (2%)
    pallas_call x1, Pallas kernels, per_device(): pl.pallas_call(functools.partial(kernel, n_expert, n_group), out_shape=ja...  31 us
    unnamed x1, local copies, waits for them, and re-layouts  0.65 us

profile of v1, /device:TPU:0, one launch (start us, length us, event | category | flops | bytes accessed | tf_op | source)
XLA Modules:
  0.0 31.6 jit_solution(10593841276016279806)
XLA Ops:
  0.0 31.0 %shard_map.73 = bf16[16,3584]{1,0:T(8,128)(2,1)S(1)} custom-call(bf16[16,7168]{1,0:T(8,128)(2,1)} %tokens.1, s32[8,16]{1,0:T(8,128)} %bitcast.2, bf16[8,16]{1,0:T(8,128)(2,1)} %bitcast.3, bf16[1,7168,2,512]{3,2,1,0:T(2,128)(2,1)} %gate_up.1, bf16[1,512,7168]{2,1,0:T(8,128)(2,1)} %down.1, bf16[3584,2,512]{2,1,0:T(2,128)(2,1)} %shared_gate_up.1, ...), custom_call_target="tpu_custom_call" | custom-call | tf_op jit(solution)/shard_map/pallas_call | solution.py:401
  31.0 0.6 %copy.9 = bf16[16,3584]{1,0:T(8,128)(2,1)} copy(bf16[16,3584]{1,0:T(8,128)(2,1)S(1)} %shard_map.73) | data formatting | bytes 229376

commit v2 on v1

v2 whole, which is shorter than its diff:
```python
import functools

import jax
import jax.numpy as jnp
from jax import lax
from jax.experimental import pallas as pl
from jax.experimental.pallas import tpu as pltpu
from jax.sharding import PartitionSpec as P

MESH = pl.DeviceIdType.MESH
BF16, F32 = jnp.bfloat16, jnp.float32
CAP = 2
LANES = 128
DEPTH = 1792
scope = jax.named_scope


def line_order(count):
    orders, stages = [], [[] for _ in range(count)]
    for me in range(count):
        others = [j for j in range(count) if j != me]
        orders.append([me] + sorted(others, key=lambda j: me - j if j < me else j - me + 1.5))
    for k in range(1, count):
        lists = []
        for me in range(count):
            blocks = []
            for j in sorted(range(count), key=lambda j: abs(j - me)):
                turn = orders[me].index(j)
                if j != me and k == (min(turn, abs(j - me)) if 0 < me < count - 1 else turn):
                    blocks.append(j)
            lists.append(blocks)
        for i in range(max(len(blocks) for blocks in lists)):
            stages[k].append([blocks[i] if i < len(blocks) else -1 for blocks in lists])
    return [[orders[me][k] for me in range(count)] for k in range(count)], stages


def choose(table, me):
    value = jnp.int32(0)
    for j, entry in enumerate(table):
        value = value + jnp.where(me == j, entry, 0)
    return value


def silu(value):
    return value / (1.0 + jnp.exp(-value))


def kernel(
    n_expert, n_group,
    tokens, ids_hbm, gates_hbm, gate_up, down, shared_gate_up, shared_down,
    out,
    w_routed, w_down, w_shared, w_shared_down,
    ids_all, gates,
    x_all, x_shared, rows_out, rows_all, x_routed,
    pre_own, pre_out, pre_in, term_out, term_in, routed_out, routed_in,
    routed_w_sem, down_w_sem, shared_w_sem, shared_down_w_sem, own_sem, ids_sem, gates_sem,
    ready, x_send, x_recv, relay_send, rows_send, rows_recv, pre_send, pre_recv,
    term_send, term_recv, routed_send, routed_recv,
):
    me_e, me_g = lax.axis_index("expert"), lax.axis_index("group")
    n_tokens, width = tokens.shape
    columns = x_all.shape[2]
    units = w_shared_down.shape[0]
    tiles = units // LANES
    pair = 2 if tiles % 2 == 0 else 1
    parts = 2 if columns % (2 * LANES) == 0 else 1
    part = columns // parts
    chunks = [pl.ds(c * part, part) for c in range(parts)]
    x_parts = x_recv.shape[1] - 1
    x_part = columns // x_parts
    x_chunks = [pl.ds(c * x_part, x_part) for c in range(x_parts)]
    order, stages = line_order(n_group)
    sources = [choose(table, me_g) for table in order]

    def expert_at(distance):
        return lax.rem(me_e + n_expert + distance, n_expert)

    def group_at(distance):
        return lax.rem(me_g + n_group + distance, n_group)

    has_left, has_right = me_g > 0, me_g < n_group - 1
    barrier = pltpu.get_barrier_semaphore()
    for d in range(1, n_expert):
        pl.semaphore_signal(barrier, inc=1, device_id={"expert": expert_at(d)}, device_id_type=MESH)

    @pl.when(has_right)
    def _():
        pl.semaphore_signal(barrier, inc=1, device_id={"group": me_g + 1}, device_id_type=MESH)

    own_columns = pl.ds(pl.multiple_of(me_e * columns, LANES), columns)
    own_copy = pltpu.make_async_copy(tokens.at[:, own_columns], x_all.at[me_g], own_sem)
    ids_copy = pltpu.make_async_copy(ids_hbm, ids_all.at[me_g], ids_sem)
    gates_copy = pltpu.make_async_copy(gates_hbm, gates, gates_sem)
    for copy in (own_copy, ids_copy, gates_copy):
        copy.start()

    def weight_copies(source, target, sem, first, at, count):
        depth = min(DEPTH, count)
        groups = []
        for n in range(count // depth):
            rows = pl.ds(pl.multiple_of(first + n * depth, LANES), depth)
            landed = pl.ds(at + n * depth, depth)
            copies = [
                pltpu.make_async_copy(
                    source.at[rows, pl.ds(c * LANES, LANES)], target.at[c, landed], sem.at[at // depth + n]
                )
                for c in range(tiles)
            ]
            whole = target.at[:, landed]
            groups.append((copies, pltpu.make_async_copy(whole, whole, sem.at[at // depth + n])))
        return groups

    half = 2 * columns
    shared_groups = weight_copies(
        shared_gate_up.reshape(half, units), w_shared, shared_w_sem, 0, 0, half
    )
    routed_groups = [
        weight_copies(
            gate_up.reshape(2 * width, units), w_routed, routed_w_sem, expert_at(h) * half, h * half, half
        )
        for h in range(n_expert)
    ]
    shared_down_copy = pltpu.make_async_copy(shared_down, w_shared_down, shared_down_w_sem)
    down_copies = [
        pltpu.make_async_copy(
            down.at[0, :, pl.ds(pl.multiple_of(expert_at(-d) * columns, LANES), columns)],
            w_down.at[d],
            down_w_sem.at[d],
        )
        for d in range(n_expert)
    ]
    with scope("own"):
        own_copy.wait()
    for copies, _ in shared_groups:
        for copy in copies:
            copy.start()
    shared_down_copy.start()
    with scope("bar"):
        pl.semaphore_wait(barrier, n_expert - 1 + jnp.where(has_left, 1, 0))

    @pl.when(has_left)
    def _():
        pl.semaphore_signal(ready, inc=1, device_id={"group": me_g - 1}, device_id_type=MESH)

    with scope("ids"):
        ids_copy.wait()

    def x_copy(source, target, c, send_sem):
        ref = x_all.at[source, :, x_chunks[c]] if c < x_parts else ids_all.at[source]
        return pltpu.make_async_remote_copy(
            src_ref=ref, dst_ref=ref, send_sem=send_sem, recv_sem=x_recv.at[source, c],
            device_id={"group": target}, device_id_type=MESH,
        )

    sends = []
    for i, (step, exists) in enumerate(((-1, has_left), (1, has_right))):
        if step > 0:
            with scope("ready1"):
                @pl.when(exists)
                def _():
                    pl.semaphore_wait(ready, 1)
        for c in range(x_parts + 1):
            pl.when(exists)(x_copy(me_g, me_g + step, c, x_send.at[i, c // x_parts]).start)
        sends.append((exists, x_send.at[i]))

    before = (
        lax.broadcasted_iota(jnp.int32, (n_tokens, n_tokens), 0)
        < lax.broadcasted_iota(jnp.int32, (n_tokens, n_tokens), 1)
    ).astype(BF16)
    ranks = lax.broadcasted_iota(jnp.int32, (8, n_tokens), 0).astype(F32)

    def picked_by(ids, expert):
        chosen = ids == expert
        named = jnp.sum(jnp.where(chosen, 1.0, 0.0), axis=0, keepdims=True)
        named = jnp.broadcast_to(named, (8, n_tokens))
        rank = jnp.dot(named.astype(BF16), before, preferred_element_type=F32)
        picked = jnp.where((named > 0.5) & (jnp.abs(rank - ranks) < 0.5), 1.0, 0.0)
        return picked, chosen

    feature = lax.broadcasted_iota(jnp.int32, (LANES, 4 * LANES), 0)
    place = lax.broadcasted_iota(jnp.int32, (LANES, 4 * LANES), 1)
    spread = (
        (place == 2 * feature) | (place == 2 * feature + 1 + 2 * LANES)
    ).astype(BF16)

    def expand(pieces, target):
        rows = pieces[0].shape[0]
        stacked = jnp.concatenate(pieces, axis=0).astype(BF16)
        both = jnp.dot(stacked, spread, preferred_element_type=F32).astype(BF16)
        for j in range(len(pieces)):
            at = pl.ds(j * 2 * LANES, 2 * LANES)
            target[:rows, at] = both[j * rows : (j + 1) * rows, : 2 * LANES]
            target[rows:, at] = both[j * rows : (j + 1) * rows, 2 * LANES :]

    def project(x, weights, groups, wait, first=0):
        depth = min(DEPTH, x.shape[1]) if wait else x.shape[1]
        totals = [None] * (tiles // pair)
        for n in range(x.shape[1] // depth):
            if wait:
                with scope(f"w{n}"):
                    groups[n][1].wait()
            rows = pl.ds(first + n * depth, depth)
            x_part = x[:, pl.ds(n * depth, depth)]
            for p in range(tiles // pair):
                block = [weights[p * pair + i, rows] for i in range(pair)]
                block = jnp.concatenate(block, axis=1) if pair > 1 else block[0]
                product = jnp.dot(x_part, block, preferred_element_type=F32)
                totals[p] = product if totals[p] is None else totals[p] + product
        return totals

    pre_copies = {}

    def pre(k):
        source = sources[k]
        with scope(f"exp{k}"):
          expand([x_all[source, :, pl.ds(j * LANES, LANES)] for j in range(columns // LANES)], x_shared)
        with scope(f"proj{k}"):
            totals = project(x_shared, w_shared, shared_groups, k == 0)
        for p, total in enumerate(totals):
            at = pl.ds(p * pair * LANES, pair * LANES)
            pre_own[k, :, at] = total
            pre_out[k, :, at] = total.astype(BF16)
        pre_copies[k] = []
        for d in range(1, n_expert):
            copy = pltpu.make_async_remote_copy(
                src_ref=pre_out.at[k], dst_ref=pre_in.at[d - 1, k],
                send_sem=pre_send.at[d - 1], recv_sem=pre_recv.at[d - 1, k],
                device_id={"expert": expert_at(d)}, device_id_type=MESH,
            )
            copy.start()
            pre_copies[k].append(copy)

    def fin(k):
        with scope(f"prew{k}"):
            for copy in pre_copies[k]:
                copy.wait_recv()
        total = pre_own[k]
        for d in range(1, n_expert):
            total = total + pre_in[d - 1, k].astype(F32)
        hidden = (silu(total[:n_tokens]) * total[n_tokens:]).astype(BF16)
        for c in range(parts):
            term = jnp.dot(hidden, w_shared_down[:, chunks[c]], preferred_element_type=F32)
            if k:
                term_out[k, :, chunks[c]] = term.astype(BF16)
                copy = pltpu.make_async_remote_copy(
                    src_ref=term_out.at[k, :, chunks[c]], dst_ref=term_in.at[me_g, :, chunks[c]],
                    send_sem=term_send, recv_sem=term_recv.at[me_g],
                    device_id={"group": sources[k]}, device_id_type=MESH,
                )
                copy.start()
            else:
                term_in[me_g, :, chunks[c]] = term.astype(BF16)

    pre(0)

    for groups in routed_groups:
        for copies, _ in groups:
            for copy in copies:
                copy.start()
    for copy in down_copies:
        copy.start()

    def arrive(k):
        for c in range(x_parts + 1):
            for i, table in enumerate(stages[k]):
                block = choose(table, me_g)
                passed = (block >= 0) & has_left & has_right
                target = jnp.where(block > me_g, me_g - 1, me_g + 1)
                sem = relay_send.at[sum(len(tables) for tables in stages[:k]) + i]
                relay = x_copy(block, target, c, sem.at[c // x_parts])
                with scope(f"x{k}{i}{c}"):
                    pl.when(block >= 0)(relay.wait_recv)
                pl.when(passed)(relay.start)
                if c == 0:
                    sends.append((passed, sem))


    def select(k):
        source = sources[k]
        picked = jnp.concatenate(
            [picked_by(ids_all[source], expert_at(d))[0] for d in range(n_expert)], axis=0
        ).astype(BF16)
        rows = jnp.dot(picked, x_all[source], preferred_element_type=F32)
        for d in range(n_expert):
            target = rows_out.at[d, k] if d else rows_all.at[0, k]
            target[...] = rows[d * 8 : d * 8 + CAP].astype(BF16)
        for d in range(1, n_expert):
            copy = pltpu.make_async_remote_copy(
                src_ref=rows_out.at[d, k], dst_ref=rows_all.at[n_expert - d, k],
                send_sem=rows_send.at[d], recv_sem=rows_recv.at[d],
                device_id={"expert": expert_at(d)}, device_id_type=MESH,
            )
            copy.start()

    routed_rows = n_group * CAP
    routed_totals = [None] * (tiles // pair)

    def project_rows(h):
        x = x_routed.at[min(h, 1)]
        with scope(f"rexp{h}"):
            pieces = [
                rows_all[h, :, :, pl.ds(j * LANES, LANES)].reshape(routed_rows, LANES).astype(F32)
                for j in range(columns // LANES)
            ]
            expand(pieces, x)
        with scope(f"rproj{h}"):
            totals = project(x, w_routed, routed_groups[h], True, h * half)
        for p, total in enumerate(totals):
            routed_totals[p] = total if routed_totals[p] is None else routed_totals[p] + total

    for k in range(1, n_group):
        arrive(k)
        pre(k)
        with scope("select"):
            if k == 1:
                select(0)
            select(k)
        if k == 2:
            shared_down_copy.wait()
        if k > 1:
            fin(k - 1)
        if k == n_group - 1:
            project_rows(0)
    if n_group < 3:
        shared_down_copy.wait()
    if n_group < 2:
        select(0)
        project_rows(0)
    else:
        fin(n_group - 1)
    with scope("rows"):
        for d in range(1, n_expert):
            rows = rows_all.at[n_expert - d]
            pltpu.make_async_remote_copy(
                src_ref=rows, dst_ref=rows, send_sem=rows_send.at[d], recv_sem=rows_recv.at[d],
                device_id={"expert": expert_at(d)}, device_id_type=MESH,
            ).wait_recv()
    for h in range(1, n_expert):
        project_rows(h)
    routed_hidden = jnp.concatenate(
        [(silu(t[:routed_rows]) * t[routed_rows:]).astype(BF16) for t in routed_totals], axis=1
    )

    for d in reversed(range(n_expert)):
        with scope(f"dw{d}"):
            down_copies[d].wait()
        for c in range(parts):
            term = jnp.dot(
                routed_hidden, w_down[d, :, chunks[c]], preferred_element_type=F32
            ).astype(BF16)
            for k in range(n_group):
                rows = term[k * CAP : (k + 1) * CAP]
                if d or k:
                    routed_out[d, k, :, chunks[c]] = rows
                else:
                    routed_in[0, me_g, :, chunks[c]] = rows
        for k in list(range(1, n_group)) + [0]:
            if d or k:
                copy = pltpu.make_async_remote_copy(
                    src_ref=routed_out.at[d, k], dst_ref=routed_in.at[d, me_g],
                    send_sem=routed_send.at[d], recv_sem=routed_recv.at[d],
                    device_id={"expert": expert_at(-d), "group": sources[k]},
                    device_id_type=MESH,
                )
                copy.start()
    fin(0)

    identity = (
        lax.broadcasted_iota(jnp.int32, (n_tokens, n_tokens), 0)
        == lax.broadcasted_iota(jnp.int32, (n_tokens, n_tokens), 1)
    ).astype(BF16)
    gates_copy.wait()
    weights = []
    for d in range(n_expert):
        picked, chosen = picked_by(ids_all[me_g], expert_at(d))
        value = jnp.sum(jnp.where(chosen, gates[...].astype(F32), 0.0), axis=0, keepdims=True)
        weights.append(lax.dot_general(
            identity, (picked * value).astype(BF16), (((1,), (1,)), ((), ())),
            preferred_element_type=F32,
        ))

    def came(ref, sem):
        return pltpu.make_async_remote_copy(
            src_ref=ref, dst_ref=ref, send_sem=sem, recv_sem=sem,
            device_id={"group": group_at(1)}, device_id_type=MESH,
        )

    for s in range(n_group):
        with scope(f"term0{s}"):
            pl.when(me_g != s)(came(term_in.at[s], term_recv.at[s]).wait_recv)
    with scope("routed"):
        for d in range(1, n_expert):
            came(routed_in.at[d], routed_recv.at[d]).wait_recv()
        if n_group > 1:
            came(routed_in.at[0, pl.ds(1, n_group - 1)], routed_recv.at[0]).wait_recv()
    for c in range(parts):
        at = chunks[c]
        total = term_in[0, :, at].astype(F32)
        for s in range(1, n_group):
            total = total + term_in[s, :, at].astype(F32)
        for d in range(n_expert):
            rows = routed_in[d, 0, :, at].astype(F32)
            for s in range(1, n_group):
                rows = rows + routed_in[d, s, :, at].astype(F32)
            for r in range(CAP):
                total = total + weights[d][:, r : r + 1] * rows[r : r + 1]
        out[:, at] = total.astype(BF16)

    with scope("sendw"):
        for exists, sem in sends:
            pl.when(exists)(came(x_all.at[0], sem.at[0]).wait_send)
            pl.when(exists)(came(ids_all.at[0], sem.at[1]).wait_send)
        for d in range(1, n_expert):
            came(rows_out.at[d], rows_send.at[d]).wait_send()
            came(pre_out, pre_send.at[d - 1]).wait_send()
            came(routed_out.at[d], routed_send.at[d]).wait_send()
        if n_group > 1:
            came(term_out.at[pl.ds(1, n_group - 1)], term_send).wait_send()
            came(routed_out.at[0, pl.ds(1, n_group - 1)], routed_send.at[0]).wait_send()


def per_device(n_expert, n_group, tokens, ids, gates, gate_up, down, shared_gate_up, shared_down):
    n_tokens, width = tokens.shape
    columns, _, units = shared_gate_up.shape
    tiles = units // LANES
    top = ids.shape[1]
    parts = 2 if columns % (2 * LANES) == 0 else 1
    n_stages = max(1, sum(len(tables) for tables in line_order(n_group)[1]))
    vmem, dma = pltpu.VMEM, pltpu.SemaphoreType.DMA
    in_vmem, in_hbm = pl.BlockSpec(memory_space=pltpu.VMEM), pl.BlockSpec(memory_space=pltpu.HBM)
    return pl.pallas_call(
        functools.partial(kernel, n_expert, n_group),
        out_shape=jax.ShapeDtypeStruct((n_tokens, columns), BF16),
        in_specs=[in_hbm] * 7,
        out_specs=in_vmem,
        scratch_shapes=[
            vmem((tiles, 2 * width, LANES), BF16),
            vmem((n_expert, units, columns), BF16),
            vmem((tiles, 2 * columns, LANES), BF16),
            vmem((units, columns), BF16),
            vmem((n_group, top, n_tokens), jnp.int32),
            vmem((top, n_tokens), BF16),
            vmem((n_group, n_tokens, columns), BF16),
            vmem((2 * n_tokens, 2 * columns), BF16),
            vmem((n_expert, n_group, CAP, columns), BF16),
            vmem((n_expert, n_group, CAP, columns), BF16),
            vmem((2, 2 * n_group * CAP, 2 * columns), BF16),
            vmem((n_group, 2 * n_tokens, units), F32),
            vmem((n_group, 2 * n_tokens, units), BF16),
            vmem((max(1, n_expert - 1), n_group, 2 * n_tokens, units), BF16),
            vmem((n_group, n_tokens, columns), BF16),
            vmem((n_group, n_tokens, columns), BF16),
            vmem((n_expert, n_group, CAP, columns), BF16),
            vmem((n_expert, n_group, CAP, columns), BF16),
            dma((2 * width // min(DEPTH, 2 * columns),)),
            dma((n_expert,)),
            dma((2 * columns // min(DEPTH, 2 * columns),)),
            dma, dma, dma, dma,
            pltpu.SemaphoreType.REGULAR,
            dma((2, 2)), dma((n_group, parts + 1)), dma((n_stages, 2)),
            dma((n_expert,)), dma((n_expert,)),
            dma((max(1, n_expert - 1),)), dma((max(1, n_expert - 1), n_group)),
            dma, dma((n_group,)),
            dma((n_expert,)), dma((n_expert,)),
        ],
        compiler_params=pltpu.CompilerParams(
            collective_id=0, has_side_effects=True, vmem_limit_bytes=42 * 2**20
        ),
    )(*(
        pltpu.with_memory_space_constraint(array, pltpu.HBM)
        for array in (tokens, ids.T, gates.T, gate_up, down, shared_gate_up, shared_down)
    ))


def solution(mesh):
    in_specs = (
        P(("dp", "group"), None),
        P(("dp", "group"), None),
        P(("dp", "group"), None),
        P("expert", None, None, "group"),
        P("expert", "group", None),
        P("expert", None, "group"),
        P("group", "expert"),
    )
    return jax.shard_map(
        functools.partial(per_device, mesh.shape["expert"], mesh.shape["group"]),
        mesh=mesh, in_specs=in_specs, out_specs=P(("dp", "group"), "expert"), check_vma=False,
    )
```

time: 31.8 us -> 30.1 us (0.947)
  Pallas kernels: 31 us -> 29.3 us
    pallas_call x1, Pallas kernels: 31 us -> 29.3 us  [per_device(): pl.pallas_call(functools.partial(kernel, n_expert, n_group), out_shape=ja...]
where the time goes in v2:
time: 30.1 us; the launch traced here: 30 us
  Pallas kernels  29.3 us (97%)
  local copies, waits for them, and re-layouts  0.65 us (2%)
    pallas_call x1, Pallas kernels, per_device(): pl.pallas_call(functools.partial(kernel, n_expert, n_group), out_shape=ja...  29.3 us
    unnamed x1, local copies, waits for them, and re-layouts  0.65 us

profile of v2, /device:TPU:0, one launch (start us, length us, event | category | flops | bytes accessed | tf_op | source)
XLA Modules:
  0.0 30.0 jit_solution(5195635672742432005)
XLA Ops:
  0.0 29.3 %shard_map.73 = bf16[16,3584]{1,0:T(8,128)(2,1)S(1)} custom-call(bf16[16,7168]{1,0:T(8,128)(2,1)} %tokens.1, s32[8,16]{1,0:T(8,128)} %bitcast.2, bf16[8,16]{1,0:T(8,128)(2,1)} %bitcast.3, bf16[1,7168,2,512]{3,2,1,0:T(2,128)(2,1)} %gate_up.1, bf16[1,512,7168]{2,1,0:T(8,128)(2,1)} %down.1, bf16[3584,2,512]{2,1,0:T(2,128)(2,1)} %shared_gate_up.1, ...), custom_call_target="tpu_custom_call" | custom-call | tf_op jit(solution)/shard_map/pallas_call | solution.py:431
  29.3 0.6 %copy.9 = bf16[16,3584]{1,0:T(8,128)(2,1)} copy(bf16[16,3584]{1,0:T(8,128)(2,1)S(1)} %shard_map.73) | data formatting | bytes 229376

commit v3 on v2

--- a/solution.py
+++ b/solution.py
@@ -94,6 +94,12 @@
     for copy in (own_copy, ids_copy, gates_copy):
         copy.start()
 
+    with scope("bar"):
+        @pl.when(has_left)
+        def _():
+            pl.semaphore_wait(barrier, n_expert)
+            pl.semaphore_signal(ready, inc=1, device_id={"group": me_g - 1}, device_id_type=MESH)
+
     def weight_copies(source, target, sem, first, at, count):
         depth = min(DEPTH, count)
         groups = []
@@ -135,12 +141,10 @@
         for copy in copies:
             copy.start()
     shared_down_copy.start()
-    with scope("bar"):
-        pl.semaphore_wait(barrier, n_expert - 1 + jnp.where(has_left, 1, 0))
-
-    @pl.when(has_left)
-    def _():
-        pl.semaphore_signal(ready, inc=1, device_id={"group": me_g - 1}, device_id_type=MESH)
+    with scope("bar0"):
+        @pl.when(me_g == 0)
+        def _():
+            pl.semaphore_wait(barrier, n_expert - 1)
 
     with scope("ids"):
         ids_copy.wait()
@@ -230,6 +234,10 @@
             copy.start()
             pre_copies[k].append(copy)
 
+    last = n_group - 1
+    swapped = sources[last] < sources[last - 1]
+    held = []
+
     def fin(k):
         with scope(f"prew{k}"):
             for copy in pre_copies[k]:
@@ -247,7 +255,11 @@
                     send_sem=term_send, recv_sem=term_recv.at[me_g],
                     device_id={"group": sources[k]}, device_id_type=MESH,
                 )
-                copy.start()
+                if 1 < k + 1 == last:
+                    pl.when(~swapped)(copy.start)
+                    held.append(copy)
+                else:
+                    copy.start()
             else:
                 term_in[me_g, :, chunks[c]] = term.astype(BF16)
 
@@ -327,7 +339,9 @@
         select(0)
         project_rows(0)
     else:
-        fin(n_group - 1)
+        fin(last)
+        for copy in held:
+            pl.when(swapped)(copy.start)
     with scope("rows"):
         for d in range(1, n_expert):
             rows = rows_all.at[n_expert - d]
@@ -354,15 +368,18 @@
                     routed_out[d, k, :, chunks[c]] = rows
                 else:
                     routed_in[0, me_g, :, chunks[c]] = rows
-        for k in list(range(1, n_group)) + [0]:
-            if d or k:
-                copy = pltpu.make_async_remote_copy(
-                    src_ref=routed_out.at[d, k], dst_ref=routed_in.at[d, me_g],
-                    send_sem=routed_send.at[d], recv_sem=routed_recv.at[d],
-                    device_id={"expert": expert_at(-d), "group": sources[k]},
-                    device_id_type=MESH,
-                )
+        for s in range(n_group):
+            slot = choose([[row[me] for row in order].index(s) for me in range(n_group)], me_g)
+            copy = pltpu.make_async_remote_copy(
+                src_ref=routed_out.at[d, slot], dst_ref=routed_in.at[d, me_g],
+                send_sem=routed_send.at[d], recv_sem=routed_recv.at[d],
+                device_id={"expert": expert_at(-d), "group": s},
+                device_id_type=MESH,
+            )
+            if d:
                 copy.start()
+            else:
+                pl.when(me_g != s)(copy.start)
     fin(0)
 
     identity = (

time: 30.1 us -> 29.7 us (0.987)
  Pallas kernels: 29.3 us -> 28.9 us
    pallas_call x1, Pallas kernels: 29.3 us -> 28.9 us  [per_device(): pl.pallas_call(functools.partial(kernel, n_expert, n_group), out_shape=ja...]
where the time goes in v3:
time: 29.7 us; the launch traced here: 29.6 us
  Pallas kernels  28.9 us (97%)
  local copies, waits for them, and re-layouts  0.65 us (2%)
    pallas_call x1, Pallas kernels, per_device(): pl.pallas_call(functools.partial(kernel, n_expert, n_group), out_shape=ja...  28.9 us
    unnamed x1, local copies, waits for them, and re-layouts  0.65 us

profile of v3, /device:TPU:0, one launch (start us, length us, event | category | flops | bytes accessed | tf_op | source)
XLA Modules:
  0.0 29.6 jit_solution(4419003345769966434)
XLA Ops:
  0.0 28.9 %shard_map.73 = bf16[16,3584]{1,0:T(8,128)(2,1)S(1)} custom-call(bf16[16,7168]{1,0:T(8,128)(2,1)} %tokens.1, s32[8,16]{1,0:T(8,128)} %bitcast.2, bf16[8,16]{1,0:T(8,128)(2,1)} %bitcast.3, bf16[1,7168,2,512]{3,2,1,0:T(2,128)(2,1)} %gate_up.1, bf16[1,512,7168]{2,1,0:T(8,128)(2,1)} %down.1, bf16[3584,2,512]{2,1,0:T(2,128)(2,1)} %shared_gate_up.1, ...), custom_call_target="tpu_custom_call" | custom-call | tf_op jit(solution)/shard_map/pallas_call | solution.py:448
  29.0 0.6 %copy.9 = bf16[16,3584]{1,0:T(8,128)(2,1)} copy(bf16[16,3584]{1,0:T(8,128)(2,1)S(1)} %shard_map.73) | data formatting | bytes 229376
